TPU v7x, 128 devices: a whole 4x4x4 slice. The times are simulated.
128 devices in a mesh: pts: 128 (over z, y, x, core).
Axes of the slice: x: 4, y: 4, z: 4, core: 2. Of those that a mesh axis runs over, the one named last changes fastest.
Arguments:
- points: bfloat16 [65536, 64], P('pts'), may hold values from -10 to 10, as said below
- targets: float32 [65536], P('pts'), may hold values from -6 to 6
- ridge_weight: float32 [], replicated, may hold values from 0.5 to 4
Outputs:
- coefficients: float32 [65536], P('pts')
- residual: float32 [65536], P('pts')
Inputs may be any that keep to these rules, and one draw needn't show every extreme that they name: `points`: each point lies near one of 1365 cluster centres; every coordinate is within -10 and 10.
All inputs are finite; a program needn't handle non-finite values.
Results may differ from a plain program's by a relative error of at most 0.005.
Values may be sent and summed in bfloat16 or wider, within the bound.
A program may use at most 192 MiB of HBM per device.

v0:
```python
import jax
import jax.numpy as jnp
from jax import lax
from jax.sharding import PartitionSpec as P

ITERS = 2


def over_all(shard, axis, dim, absorb, state):
    everything = jax.tree.map(lambda a: lax.all_gather(a, axis, axis=dim, tiled=True), shard)
    return absorb(state, everything, jnp.int32(0))


def kernel_times(own_points, own_norms, shard_rows, coef_part, inverse_width):
    widened = shard_rows.astype(jnp.float32)
    shard_norms = jnp.sum(widened * widened, axis=1)
    cross_term = jnp.dot(own_points, shard_rows.T, preferred_element_type=jnp.float32)
    distance = own_norms[:, None] + shard_norms[None, :] - 2.0 * cross_term
    kernel = jnp.exp(-inverse_width * distance).astype(jnp.bfloat16)
    return jnp.dot(kernel, coef_part, preferred_element_type=jnp.float32)


def apply_operator(direction, points, own_norms, ridge_weight, inverse_width):
    coef_whole = lax.all_gather(direction, "pts", axis=0, tiled=True).astype(jnp.bfloat16)
    local_rows = points.shape[0]
    empty = jnp.zeros((local_rows,), jnp.float32)

    def accumulate(running, shard_rows, first_row):
        coef_part = lax.dynamic_slice_in_dim(coef_whole, first_row, shard_rows.shape[0], 0)
        return running + kernel_times(points, own_norms, shard_rows, coef_part, inverse_width)

    summed = over_all(points, "pts", 0, accumulate, empty)
    return summed + ridge_weight * direction


def body(points, targets, ridge_weight):
    inverse_width = 1.0 / points.shape[1]
    widened = points.astype(jnp.float32)
    own_norms = jnp.sum(widened * widened, axis=1)
    coefficients = jnp.zeros_like(targets)
    residual = targets
    direction = targets
    norm_now = lax.psum(jnp.sum(residual * residual), "pts")
    for iteration in range(ITERS):
        applied = apply_operator(direction, points, own_norms, ridge_weight, inverse_width)
        curvature = lax.psum(jnp.sum(direction * applied), "pts")
        step_size = norm_now / curvature
        coefficients = coefficients + step_size * direction
        residual = residual - step_size * applied
        if iteration + 1 < ITERS:
            norm_next = lax.psum(jnp.sum(residual * residual), "pts")
            direction = residual + norm_next / norm_now * direction
            norm_now = norm_next
    return (coefficients, residual)


def solution(mesh):
    in_specs = (P("pts", None), P("pts"), P())
    out_specs = (P("pts"), P("pts"))
    return jax.shard_map(body, mesh=mesh, in_specs=in_specs, out_specs=out_specs, check_vma=False)
```

profile of v0, /device:TPU:1, one launch (start us, length us, event | category | flops | bytes accessed | tf_op | source)
XLA Modules:
  0.0 421.1 jit_solution(7637829127541475642)
XLA Ops:
  7.2 0.0 all-gather.4.cloned.1.call-start
  7.2 0.7 all-gather.4.cloned.1.call-update
  7.9 0.7 convert
  9.2 38.9 %all-gather = bf16[128,1,512]{2,1,0:T(2,128)(2,1)S(1)} all-gather(bf16[1,1,512]{2,1,0:T(2,128)(2,1)S(1)} %convert), channel_id=1, replica_groups=mesh['pts'=128] {'pts'}, dimensions={0}, use_global_device_ids=true | all-gather | bytes 132096 | tf_op jit(solution)/shard_map/all_gather | solution.py:24
  48.1 0.9 multiply_reduce_fusion.1
  49.0 39.0 %all-gather.4.cloned.1.call-done = bf16[65536,64]{0,1:T(8,128)(2,1)} async-done(((bf16[512,64]{0,1:T(8,128)(2,1)}), bf16[65536,64]{0,1:T(8,128)(2,1)}) %all-gather.4.cloned.1.call-update) | async-done | bytes 8388624 | tf_op jit(solution)/shard_map/all_gather | solution.py:10
  88.0 5.4 %multiply_reduce_fusion = f32[65536]{0:T(1024)S(1)} fusion(bf16[65536,64]{0,1:T(8,128)(2,1)} %all-gather.4.cloned.1.call-done), kind=kLoop, calls=%fused_computation.1 | loop fusion | flops 12517376 | bytes 8650752 | tf_op jit(solution)/shard_map/reduce_sum | solution.py:16
  93.4 36.7 %exponential_convert_fusion = bf16[512,65536]{1,0:T(8,128)(2,1)} fusion(bf16[512,64]{0,1:T(8,128)(2,1)} %param.3, bf16[65536,64]{0,1:T(8,128)(2,1)} %all-gather.4.cloned.1.call-done, f32[65536]{0:T(1024)S(1)} %multiply_reduce_fusion, f32[512]{0:T(512)S(1)} %multiply_reduce_fusion.1), kind=kOutput, calls=%fused_computation | convolution fusion | flops 4462739456 | bytes 75827200 | tf_op jit(solution)/shard_map/dot_general | solution.py:17
  130.1 0.0 copy-start
  130.1 26.6 %fusion = f32[1,512]{1,0:T(1,128)S(1)} fusion(bf16[512,65536]{1,0:T(8,128)(2,1)} %exponential_convert_fusion, bf16[65536,1]{0,1:T(2,128)(2,1)S(1)} %bitcast.12), kind=kOutput, calls=%fused_computation.13 | convolution fusion | flops 67108864 | bytes 67241984 | tf_op jit(solution)/shard_map/dot_general | solution.py:20
  156.7 0.0 copy-done
  156.7 0.6 multiply_reduce_fusion.4
  157.3 64.5 %all-reduce = (f32[]{:T(128)}, f32[]{:T(128)}) all-reduce(f32[]{:T(128)} %get-tuple-element.3, f32[]{:T(128)} %get-tuple-element.2), channel_id=1, replica_groups=mesh['pts'=128] {'pts'}, use_global_device_ids=true, to_apply=%region_1.0 | all-reduce | flops 2 | bytes 16 | tf_op jit(solution)/shard_map/psum | solution.py:43
  223.1 0.6 multiply_reduce_fusion.3
  223.7 63.8 %psum.30 = f32[]{:T(128)} all-reduce(f32[]{:T(128)} %multiply_reduce_fusion.3), channel_id=1, replica_groups=mesh['pts'=128] {'pts'}, use_global_device_ids=true, to_apply=%region_7.0 | all-reduce | flops 1 | bytes 8 | tf_op jit(solution)/shard_map/psum | solution.py:51
  288.9 34.1 %all-gather.1 = bf16[128,1,512]{2,1,0:T(2,128)(2,1)S(1)} all-gather(bf16[1,1,512]{2,1,0:T(2,128)(2,1)S(1)} %convert.1), channel_id=1, replica_groups=mesh['pts'=128] {'pts'}, dimensions={0}, use_global_device_ids=true | all-gather | bytes 132096 | tf_op jit(solution)/shard_map/all_gather | solution.py:24
  323.0 26.6 %fusion.1 = f32[1,512]{1,0:T(1,128)S(1)} fusion(bf16[512,65536]{1,0:T(8,128)(2,1)} %exponential_convert_fusion, bf16[65536,1]{0,1:T(2,128)(2,1)S(1)} %bitcast.13), kind=kOutput, calls=%fused_computation.14 | convolution fusion | flops 67108864 | bytes 67241984 | tf_op jit(solution)/shard_map/dot_general | solution.py:20
  349.6 0.6 multiply_reduce_fusion.2
  350.2 62.1 %psum.31 = f32[]{:T(128)} all-reduce(f32[]{:T(128)} %multiply_reduce_fusion.2), channel_id=1, replica_groups=mesh['pts'=128] {'pts'}, use_global_device_ids=true, to_apply=%region_9.0 | all-reduce | flops 1 | bytes 8 | tf_op jit(solution)/shard_map/psum | solution.py:46
  413.7 0.6 multiply_subtract_fusion
  (2 shorter events, 0.0 us)
Async XLA Ops:
  7.2 80.8 %all-gather.4.cloned.1.call-start = ((), (), s32[]{:S(2)}) async-start(), calls=%async_computation | async-start | bytes 8454144 | tf_op jit(solution)/shard_map/all_gather | solution.py:10
  130.1 26.6 %copy-start = (f32[512]{0:T(512)S(1)}, f32[512]{0:T(512)}, u32[]{:S(2)}) copy-start(f32[512]{0:T(512)} %param.4) | copy-start | bytes 6148
Sparse Core Ops, SparseCore 0:
  10.8 77.1 all-gather.3
where the time goes:
time: 422 us; the launch traced here: 421 us
  blocking collectives  263 us (62%)
  matrix products  89.8 us (21%)
  waiting for transfers between devices  39.7 us (9%)
  between operations  18.7 us (4%)
  other arithmetic  9.44 us (2%)
    all_gather x2, blocking collectives, apply_operator(): lax.all_gather(direction, 'pts', axis=0, tiled=True).astype(jnp.bfloat16)  73 us
    psum x1, blocking collectives, body(): norm_now = lax.psum(jnp.sum(residual * residual), 'pts')  64.5 us
    psum x1, blocking collectives, body(): norm_next = lax.psum(jnp.sum(residual * residual), 'pts')  63.8 us
    psum x1, blocking collectives, body(): curvature = lax.psum(jnp.sum(direction * applied), 'pts')  62.1 us
    dot_general x2, matrix products, kernel_times(): return jnp.dot(kernel, coef_part, preferred_element_type=jnp.float32)  53.2 us
    all_gather x1, waiting for transfers between devices, over_all(): lax.all_gather(a, axis, axis=dim, tiled=True)  39 us
    dot_general x1, matrix products, kernel_times(): jnp.dot(own_points, shard_rows.T, preferred_element_type=jnp.float32)  36.7 us
  transfers between devices with their start and end apart: 1, of which 1 were waited for; matrix products, arithmetic and copies ran while one was open for 0% of the time, Pallas kernels for 0%

commit v1 on v0

--- a/solution.py
+++ b/solution.py
@@ -4,6 +4,18 @@
 from jax.sharding import PartitionSpec as P
 
 ITERS = 2
+
+
+def types_deliver(lane_axis, incoming_x):
+    return jnp.concatenate(
+        lax.all_to_all(
+            jnp.stack(tuple((incoming_x for _ in range(lax.axis_size(lane_axis)))), axis=0),
+            lane_axis,
+            0,
+            0,
+        ),
+        axis=0,
+    )
 
 
 def over_all(shard, axis, dim, absorb, state):
@@ -21,7 +33,7 @@
 
 
 def apply_operator(direction, points, own_norms, ridge_weight, inverse_width):
-    coef_whole = lax.all_gather(direction, "pts", axis=0, tiled=True).astype(jnp.bfloat16)
+    coef_whole = types_deliver("pts", direction).astype(jnp.bfloat16)
     local_rows = points.shape[0]
     empty = jnp.zeros((local_rows,), jnp.float32)
 

time: 422 us -> 405 us (0.960)
  blocking collectives: 263 us -> 206 us
  waiting for transfers between devices: 39.7 us -> 64.3 us
  starting transfers between devices: 0.04 us -> 11.5 us
    all_gather x2 -> x0, blocking collectives: 73 us -> none  [apply_operator(): lax.all_gather(direction, 'pts', axis=0, tiled=True).astype(jnp.bfloat16)]
    all_gather x1, waiting for transfers between devices: 39 us -> 55.1 us  [over_all(): lax.all_gather(a, axis, axis=dim, tiled=True)]
    all_to_all x0 -> x1, blocking collectives: none -> 14.6 us  [types_deliver(): lax.all_to_all(jnp.stack(tuple((incoming_x for _ in range(lax.axis_size(l...]
    all_to_all x0 -> x1, starting transfers between devices: none -> 11.5 us  [types_deliver(): lax.all_to_all(jnp.stack(tuple((incoming_x for _ in range(lax.axis_size(l...]
    all_to_all x0 -> x1, waiting for transfers between devices: none -> 8.49 us  [types_deliver(): lax.all_to_all(jnp.stack(tuple((incoming_x for _ in range(lax.axis_size(l...]
  transfers between devices with their start and end apart: 1 -> 2, of which waited for: 1 -> 2; matrix products, arithmetic and copies ran while one was open for 0% -> 1% of each run, Pallas kernels for 0% -> 0%
where the time goes in v1:
time: 405 us; the launch traced here: 404 us
  blocking collectives  206 us (51%)
  matrix products  89.8 us (22%)
  waiting for transfers between devices  64.3 us (16%)
  between operations  18.8 us (5%)
  other arithmetic  11.6 us (3%)
  starting transfers between devices  11.5 us (3%)
    psum x1, blocking collectives, body(): norm_now = lax.psum(jnp.sum(residual * residual), 'pts')  64.5 us
    psum x1, blocking collectives, body(): norm_next = lax.psum(jnp.sum(residual * residual), 'pts')  63.8 us
    psum x1, blocking collectives, body(): curvature = lax.psum(jnp.sum(direction * applied), 'pts')  62.8 us
    all_gather x1, waiting for transfers between devices, over_all(): lax.all_gather(a, axis, axis=dim, tiled=True)  55.1 us
    dot_general x2, matrix products, kernel_times(): return jnp.dot(kernel, coef_part, preferred_element_type=jnp.float32)  53.2 us
    dot_general x1, matrix products, kernel_times(): jnp.dot(own_points, shard_rows.T, preferred_element_type=jnp.float32)  36.6 us
    all_to_all x1, blocking collectives, types_deliver(): lax.all_to_all(jnp.stack(tuple((incoming_x for _ in range(lax.axis_size(l...  14.6 us
    all_to_all x1, starting transfers between devices, types_deliver(): lax.all_to_all(jnp.stack(tuple((incoming_x for _ in range(lax.axis_size(l...  11.5 us
  transfers between devices with their start and end apart: 2, of which 2 were waited for; matrix products, arithmetic and copies ran while one was open for 1% of the time, Pallas kernels for 0%

profile of v1, /device:TPU:1, one launch (start us, length us, event | category | flops | bytes accessed | tf_op | source)
XLA Modules:
  0.0 404.0 jit_solution(10644098647447051688)
XLA Ops:
  7.2 0.0 all-gather.2.cloned.1.call-start
  7.2 0.7 all-gather.2.cloned.1.call-update
  7.9 0.8 stack.4
  8.7 0.5 broadcast.20
  9.2 1.4 reduce
  10.6 0.7 reshape.32
  11.3 11.5 %all-to-all-start = ((bf16[128,2,256]{2,1,0:T(2,128)(2,1)}), bf16[128,2,256]{2,1,0:T(2,128)(2,1)S(1)}, u32[]{:S(2)}, u32[]{:S(2)}) async-start(bf16[128,2,256]{2,1,0:T(2,128)(2,1)} %reshape.32), calls=%async_computation | async-start | bytes 262144 | tf_op jit(solution)/shard_map/all_to_all | solution.py:11
  23.5 0.9 multiply_reduce_fusion.1
  24.3 8.5 %all-to-all-done = bf16[128,2,256]{2,1,0:T(2,128)(2,1)S(1)} async-done(((bf16[128,2,256]{2,1,0:T(2,128)(2,1)}), bf16[128,2,256]{2,1,0:T(2,128)(2,1)S(1)}, u32[]{:S(2)}, u32[]{:S(2)}) %all-to-all-start) | async-done | bytes 131104 | tf_op jit(solution)/shard_map/all_to_all | solution.py:11
  32.8 0.1 reshape.33
  32.9 55.1 %all-gather.2.cloned.1.call-done = bf16[65536,64]{0,1:T(8,128)(2,1)} async-done(((bf16[512,64]{0,1:T(8,128)(2,1)}), bf16[65536,64]{0,1:T(8,128)(2,1)}) %all-gather.2.cloned.1.call-update) | async-done | bytes 8388624 | tf_op jit(solution)/shard_map/all_gather | solution.py:22
  88.0 5.4 %multiply_reduce_fusion = f32[65536]{0:T(1024)S(1)} fusion(bf16[65536,64]{0,1:T(8,128)(2,1)} %all-gather.2.cloned.1.call-done), kind=kLoop, calls=%fused_computation.1 | loop fusion | flops 12517376 | bytes 8650752 | tf_op jit(solution)/shard_map/reduce_sum | solution.py:28
  93.4 36.6 %exponential_convert_fusion = bf16[512,65536]{1,0:T(8,128)(2,1)} fusion(bf16[512,64]{0,1:T(8,128)(2,1)} %param.3, bf16[65536,64]{0,1:T(8,128)(2,1)} %all-gather.2.cloned.1.call-done, f32[65536]{0:T(1024)S(1)} %multiply_reduce_fusion, f32[512]{0:T(512)S(1)} %multiply_reduce_fusion.1), kind=kOutput, calls=%fused_computation | convolution fusion | flops 4462739456 | bytes 75827200 | tf_op jit(solution)/shard_map/dot_general | solution.py:29
  130.1 0.0 copy-start
  130.1 26.6 %fusion = f32[1,512]{1,0:T(1,128)S(1)} fusion(bf16[512,65536]{1,0:T(8,128)(2,1)} %exponential_convert_fusion, bf16[65536,1]{0,1:T(2,128)(2,1)S(1)} %bitcast.10), kind=kOutput, calls=%fused_computation.13 | convolution fusion | flops 67108864 | bytes 67241984 | tf_op jit(solution)/shard_map/dot_general | solution.py:32
  156.7 0.0 copy-done
  156.7 0.6 multiply_reduce_fusion.4
  157.3 64.5 %all-reduce = (f32[]{:T(128)}, f32[]{:T(128)}) all-reduce(f32[]{:T(128)} %get-tuple-element.3, f32[]{:T(128)} %get-tuple-element.2), channel_id=1, replica_groups=mesh['pts'=128] {'pts'}, use_global_device_ids=true, to_apply=%region_1.0 | all-reduce | flops 2 | bytes 16 | tf_op jit(solution)/shard_map/psum | solution.py:55
  223.2 0.6 multiply_reduce_fusion.3
  223.8 63.8 %psum.30 = f32[]{:T(128)} all-reduce(f32[]{:T(128)} %multiply_reduce_fusion.3), channel_id=1, replica_groups=mesh['pts'=128] {'pts'}, use_global_device_ids=true, to_apply=%region_7.0 | all-reduce | flops 1 | bytes 8 | tf_op jit(solution)/shard_map/psum | solution.py:63
  289.0 0.1 stack.5
  289.1 1.4 reduce.1
  290.6 14.6 %all_to_all.12 = bf16[128,2,256]{2,1,0:T(2,128)(2,1)S(1)} all-to-all(bf16[128,2,256]{2,1,0:T(2,128)(2,1)S(1)} %reshape.34), channel_id=1, replica_groups=mesh['pts'=128] {'pts'}, dimensions={0} | all-to-all | bytes 262144 | tf_op jit(solution)/shard_map/all_to_all | solution.py:11
  305.2 0.1 reshape.35
  305.3 26.6 %fusion.1 = f32[1,512]{1,0:T(1,128)S(1)} fusion(bf16[512,65536]{1,0:T(8,128)(2,1)} %exponential_convert_fusion, bf16[65536,1]{0,1:T(2,128)(2,1)S(1)} %bitcast.11), kind=kOutput, calls=%fused_computation.14 | convolution fusion | flops 67108864 | bytes 67241984 | tf_op jit(solution)/shard_map/dot_general | solution.py:32
  331.9 0.6 multiply_reduce_fusion.2
  332.5 62.8 %psum.31 = f32[]{:T(128)} all-reduce(f32[]{:T(128)} %multiply_reduce_fusion.2), channel_id=1, replica_groups=mesh['pts'=128] {'pts'}, use_global_device_ids=true, to_apply=%region_9.0 | all-reduce | flops 1 | bytes 8 | tf_op jit(solution)/shard_map/psum | solution.py:58
  396.6 0.6 multiply_subtract_fusion
  (2 shorter events, 0.0 us)
Async XLA Ops:
  7.2 80.8 %all-gather.2.cloned.1.call-start = ((), (), s32[]{:S(2)}) async-start(), calls=%async_computation.2 | async-start | bytes 8454144 | tf_op jit(solution)/shard_map/all_gather | solution.py:22
  11.3 21.5 %all-to-all-start = ((bf16[128,2,256]{2,1,0:T(2,128)(2,1)}), bf16[128,2,256]{2,1,0:T(2,128)(2,1)S(1)}, u32[]{:S(2)}, u32[]{:S(2)}) async-start(bf16[128,2,256]{2,1,0:T(2,128)(2,1)} %reshape.32), calls=%async_computation | async-start | bytes 262144 | tf_op jit(solution)/shard_map/all_to_all | solution.py:11
  130.1 26.6 %copy-start = (f32[512]{0:T(512)S(1)}, f32[512]{0:T(512)}, u32[]{:S(2)}) copy-start(f32[512]{0:T(512)} %param.4) | copy-start | bytes 6148
Sparse Core Ops, SparseCore 0:
  10.8 77.1 all-gather.1
